TPU v7x, 32 devices: a whole 2x2x4 slice. The times are simulated.
32 devices in a mesh: batch: 4 (over x, core), vocab: 8 (over z, y).
Axes of the slice: x: 2, y: 2, z: 4, core: 2. Of those that a mesh axis runs over, the one named last changes fastest.
Arguments:
- hidden_rows: bfloat16 [4096, 4096], P(('batch', 'vocab')), parts along dimension 0
- head_weight: bfloat16 [4096, 10240], P(None, 'vocab'), may hold values from -0.09375 to 0.09375
- draft_ids: int32 [64, 64], P('batch'), parts along dimension 0, may hold values from 0 to 10239
- parents: int32 [64, 64], P('batch'), parts along dimension 0, may hold values from 0 to 62, as said below
Outputs:
- log_total: float32 [64, 64], P('batch'), parts along dimension 0
- draft_logp: float32 [64, 64], P('batch'), parts along dimension 0
- path_sum: float32 [64, 64], P('batch'), parts along dimension 0
There are 4 independent parts, one for each index of `batch`. A program takes and returns all parts, laid end to end along the dimension named above; an argument that names none is the same for every part. Nothing has to cross between parts.
Inputs may be any that keep to these rules, and one draw needn't show every extreme that they name: parents[s, 0] = 0 for every sequence, and parents[s, n] lies in 0 to n - 1 for n > 0, so that every node's ancestors lead to node 0.
All inputs are finite; a program needn't handle non-finite values.
Results may differ from a plain program's by a relative error of at most 0.0003.
Values may be sent and summed in bfloat16 or wider, within the bound.
A program may use at most 128 MiB of HBM per device.

v0:
```python
import jax
import jax.numpy as jnp
from jax import lax
from jax.sharding import PartitionSpec as P


def per_device(hidden_rows, head_weight, draft_ids, parents):
    shard_width = head_weight.shape[1]
    offset = lax.axis_index("vocab") * shard_width
    gathered = lax.all_gather(hidden_rows, "vocab", axis=0, tiled=True)
    logits = jnp.dot(gathered, head_weight, preferred_element_type=jnp.float32)
    seq_count, node_count = draft_ids.shape
    node_ids = jnp.arange(node_count, dtype=jnp.int32)
    local_max = jnp.max(logits, axis=1)
    parent_rows = (jnp.arange(seq_count, dtype=jnp.int32)[:, None] * node_count + parents).reshape(
        -1
    )
    columns = draft_ids.reshape(-1) - offset
    inside = (columns >= 0) & (columns < shard_width)
    picked = jnp.take(
        logits.reshape(-1), parent_rows * shard_width + jnp.clip(columns, 0, shard_width - 1)
    )
    local_target = jnp.where(inside, picked, jnp.zeros_like(picked))
    row_top = lax.pmax(local_max, "vocab")
    local_sum = jnp.sum(jnp.exp(logits - row_top[:, None]), axis=1)
    row_total, target = lax.psum((local_sum, local_target), "vocab")
    log_total = (row_top + jnp.log(row_total)).reshape(seq_count, node_count)
    target = target.reshape(seq_count, node_count)
    choose = (parents[:, :, None] == node_ids[None, None, :]).astype(jnp.float32)
    log_parent = jnp.einsum("snr,sr->sn", choose, log_total, precision=lax.Precision.HIGHEST)
    draft_logp = jnp.where(node_ids[None, :] > 0, target - log_parent, jnp.zeros_like(target))
    path_sum = draft_logp
    jump_table = choose
    for jump_round in range((node_count - 1).bit_length()):
        path_sum = path_sum + jnp.einsum(
            "snr,sr->sn", jump_table, path_sum, precision=lax.Precision.HIGHEST
        )
        jump_table = jnp.einsum(
            "snr,srq->snq", jump_table, jump_table, precision=lax.Precision.HIGHEST
        )
    return (log_total, draft_logp, path_sum)


def solution(mesh):
    placed = (P(("batch", "vocab"), None), P(None, "vocab"), P("batch", None), P("batch", None))
    return jax.shard_map(
        per_device,
        mesh=mesh,
        in_specs=placed,
        out_specs=(P("batch", None), P("batch", None), P("batch", None)),
        check_vma=False,
    )
```

profile of v0, /device:TPU:0, one launch (start us, length us, event | category | flops | bytes accessed | tf_op | source)
XLA Modules:
  0.0 244.8 jit_solution(11728580934467642149)
XLA Ops:
  7.2 0.0 all-gather.2.cloned.1.call-start
  7.2 0.7 all-gather.2.cloned.1.call-update
  7.9 0.8 clamp_add_fusion
  8.7 0.1 add.79
  8.8 0.1 add.76
  8.9 0.7 compare_and_fusion
  9.6 0.1 and.15
  9.7 1.4 fusion
  11.1 0.6 fusion.8
  11.7 0.6 fusion.10
  12.4 0.6 fusion.12
  13.0 0.6 fusion.14
  13.7 123.6 %all-gather.2.cloned.1.call-done = bf16[1024,4096]{1,0:T(8,128)(2,1)} async-done(((bf16[128,4096]{1,0:T(8,128)(2,1)}), bf16[1024,4096]{1,0:T(8,128)(2,1)}) %all-gather.2.cloned.1.call-update) | async-done | bytes 8388624 | tf_op jit(solution)/shard_map/all_gather | solution.py:10
  137.3 18.1 %fusion.6 = (f32[1024]{0:T(1024)S(1)}, f32[1024,1280]{1,0:T(8,128)}) fusion(bf16[1024,4096]{1,0:T(8,128)(2,1)} %all-gather.2.cloned.1.call-done, bf16[4096,1280]{1,0:T(8,128)(2,1)} %param.5), kind=kOutput, calls=%fused_computation.19 | convolution fusion | flops 10738727936 | bytes 24121344 | tf_op jit(solution)/shard_map/dot_general | solution.py:11
  155.5 0.0 copy-start
  155.5 6.5 %reshape.94 = f32[1310720]{0:T(1024)} reshape(f32[1024,1280]{1,0:T(8,128)} %get-tuple-element.6) | data formatting | bytes 10485760 | tf_op jit(solution)/shard_map/reshape | solution.py:21
  162.0 13.3 %gather_fusion = f32[1024]{0:T(1024)S(1)} fusion(f32[1310720]{0:T(1024)} %reshape.94, s32[1024]{0:T(1024)S(1)} %broadcast_clamp_fusion), kind=kCustom, calls=%fused_computation | custom fusion | bytes 12288 | tf_op jit(solution)/shard_map/jit(_take)/gather | solution.py:20
  175.3 0.1 reshape.95
  175.4 18.3 %pmax.7 = f32[1024]{0:T(1024)S(1)} all-reduce(f32[1024]{0:T(1024)S(1)} %get-tuple-element.5), channel_id=1, replica_groups=mesh['batch'=4,'vocab'=8] {'vocab'}, use_global_device_ids=true, to_apply=%region_1.2 | all-reduce | flops 1024 | bytes 8192 | tf_op jit(solution)/shard_map/pmax | solution.py:24
  193.7 3.4 %exponential_reduce_fusion = f32[1024]{0:T(1024)S(1)} fusion(f32[1024,1280]{1,0:T(8,128)} %get-tuple-element.6, f32[1024]{0:T(1024)S(1)} %pmax.7), kind=kLoop, calls=%fused_computation.1 | loop fusion | flops 2620416 | bytes 5251072 | tf_op jit(solution)/shard_map/reduce_sum | solution.py:25
  197.1 33.6 %all-reduce = (f32[1024]{0:T(1024)S(1)}, f32[16,64]{1,0:T(8,128)S(1)}) all-reduce(f32[1024]{0:T(1024)S(1)} %exponential_reduce_fusion, f32[16,64]{1,0:T(8,128)S(1)} %reshape.95), channel_id=1, replica_groups=mesh['batch'=4,'vocab'=8] {'vocab'}, use_global_device_ids=true, to_apply=%region_3.4 | all-reduce | flops 2048 | bytes 16384 | tf_op jit(solution)/shard_map/psum | solution.py:26
  230.7 0.1 reshape.104
  230.8 0.7 reshape.93
  231.5 0.0 copy-done
  231.5 0.6 fusion.2
  232.1 0.0 copy-start.1
  232.1 0.6 fusion.1
  232.7 0.9 fusion.7
  233.6 0.9 fusion.9
  234.6 0.9 fusion.11
  235.5 0.9 fusion.13
  236.4 0.9 fusion.15
  237.4 0.6 add.87
  238.0 0.0 copy-done.1
  (12 shorter events, 0.1 us)
Async XLA Ops:
  7.2 130.2 %all-gather.2.cloned.1.call-start = ((), (), s32[]{:S(2)}) async-start(), calls=%async_computation | async-start | bytes 9437184 | tf_op jit(solution)/shard_map/all_gather | solution.py:10
  155.5 76.0 %copy-start = (s32[16,64]{1,0:T(8,128)S(1)}, s32[16,64]{1,0:T(8,128)}, u32[]{:S(2)}) copy-start(s32[16,64]{1,0:T(8,128)} %param.7) | copy-start | bytes 12292
  232.1 5.9 %copy-start.1 = (f32[16,64]{1,0:T(8,128)}, f32[16,64]{1,0:T(8,128)S(1)}, u32[]{:S(2)}) copy-start(f32[16,64]{1,0:T(8,128)S(1)} %subtract_select_fusion) | copy-start | bytes 12292
Sparse Core Ops, SparseCore 0:
  10.1 127.1 all-gather.1
where the time goes:
time: 246 us; the launch traced here: 245 us
  waiting for transfers between devices  124 us (50%)
  blocking collectives  52 us (21%)
  matrix products  28 us (11%)
  local copies, waits for them, and re-layouts  20.9 us (8%)
  between operations  14.1 us (6%)
  other arithmetic  5.6 us (2%)
    all_gather x1, waiting for transfers between devices, per_device(): gathered = lax.all_gather(hidden_rows, 'vocab', axis=0, tiled=True)  124 us
    psum x1, blocking collectives, per_device(): row_total, target = lax.psum((local_sum, local_target), 'vocab')  33.6 us
    pmax x1, blocking collectives, per_device(): row_top = lax.pmax(local_max, 'vocab')  18.3 us
    dot_general x1, matrix products, per_device(): logits = jnp.dot(gathered, head_weight, preferred_element_type=jnp.float32)  18.1 us
    gather x1, local copies, waits for them, and re-layouts, per_device(): jnp.take(logits.reshape(-1), parent_rows * shard_width + jnp.clip(columns...  13.3 us
    reshape x1, local copies, waits for them, and re-layouts, per_device(): logits.reshape(-1)  6.49 us
    dot_general x6, matrix products, per_device(): jnp.einsum('snr,sr->sn', jump_table, path_sum, precision=lax.Precision.HI...  5.26 us
  transfers between devices with their start and end apart: 1, of which 1 were waited for; matrix products, arithmetic and copies ran while one was open for 2% of the time, Pallas kernels for 0%

commit v1 on v0

--- a/solution.py
+++ b/solution.py
@@ -1,10 +1,20 @@
+import functools
+
 import jax
 import jax.numpy as jnp
 from jax import lax
+from jax.experimental import pallas as pl
+from jax.experimental.pallas import tpu as pltpu
 from jax.sharding import PartitionSpec as P
 
-
-def per_device(hidden_rows, head_weight, draft_ids, parents):
+MESH = pl.DeviceIdType.MESH
+LANES = 128
+TILE = 256
+SUB = 4
+CHUNKS = 4
+
+
+def general(hidden_rows, head_weight, draft_ids, parents):
     shard_width = head_weight.shape[1]
     offset = lax.axis_index("vocab") * shard_width
     gathered = lax.all_gather(hidden_rows, "vocab", axis=0, tiled=True)
@@ -41,10 +51,375 @@
     return (log_total, draft_logp, path_sum)
 
 
+def plan(tiles):
+    steps = {}
+    for t in range(tiles):
+        steps.setdefault(1 + t, []).append((0, t))
+    for t in range(tiles):
+        steps.setdefault(8 + t // 2, []).append((1, t))
+        steps.setdefault(16 + t // 2, []).append((2, t))
+    for j in range(tiles):
+        ready = SUB * j + SUB + 1
+        for o, come in ((0, 6), (1, 10), (2, 18)):
+            steps.setdefault(max(ready, come), []).append((o, tiles + j))
+    return steps
+
+
+def table(index, values):
+    out = jnp.int32(values[-1])
+    for k in range(len(values) - 2, -1, -1):
+        if values[k] != values[k + 1]:
+            out = jnp.where(index <= k, jnp.int32(values[k]), out)
+    return out
+
+
+def split3(x):
+    hi = x.astype(jnp.bfloat16)
+    rest = x - hi.astype(jnp.float32)
+    mid = rest.astype(jnp.bfloat16)
+    lo = (rest - mid.astype(jnp.float32)).astype(jnp.bfloat16)
+    return hi, mid, lo
+
+
+def kernel(n, nodes, h_ref, w_ref, draft_ref, par_ref, lt_ref, dl_ref, ps_ref,
+           rows, wv, lg, st, pick, anc, jump,
+           up_s, dn_s, r_r, y_s, y_r, x_s, x_r, d_s, d_r, st_s, st_r, loc_w, loc_r):
+    b, v = lax.axis_index("batch"), lax.axis_index("vocab")
+    x, z, y = b // 2, v // 2, v % 2
+    peers = 2 * n
+    yp = v + 1 - 2 * y
+    xb = b + 2 - 4 * x
+    cb = b + 1 - 2 * (b % 2)
+    cxb = cb + 2 - 4 * x
+    count, depth = h_ref.shape
+    width = w_ref.shape[1]
+    tiles = width // TILE
+    quarter = depth // 4
+    piece = quarter // SUB
+    part = count // CHUNKS
+    total = tiles * SUB
+    pairs = par_ref.shape[0]
+
+    barrier = pltpu.get_barrier_semaphore()
+    for k in range(1, peers):
+        pl.semaphore_signal(barrier, inc=1, device_id=(b, lax.rem(v + k, peers)), device_id_type=MESH)
+    pl.semaphore_signal(barrier, inc=1, device_id=(cb, v), device_id_type=MESH)
+    pl.semaphore_signal(barrier, inc=1, device_id=(xb, v), device_id_type=MESH)
+
+    def own_w(t):
+        return pltpu.make_async_copy(w_ref.at[:, pl.ds(t * TILE, TILE)], wv.at[t], loc_w.at[t])
+
+    own_rows = pltpu.make_async_copy(h_ref, rows.at[z], loc_r)
+    own_rows.start()
+    for t in range(tiles):
+        own_w(t).start()
+    pl.semaphore_wait(barrier, peers + 1)
+
+    def hop(src, k, there, send, own):
+        here = h_ref if own else rows.at[src]
+        cut = pl.ds(k * part, part)
+        return pltpu.make_async_remote_copy(
+            src_ref=here.at[cut], dst_ref=rows.at[src, cut],
+            send_sem=send.at[src, k], recv_sem=r_r.at[src, k],
+            device_id=(b, there), device_id_type=MESH)
+
+    def up(src, k, own=False):
+        return hop(src, k, v + 2, up_s, own)
+
+    def down(src, k, own=False):
+        return hop(src, k, v - 2, dn_s, own)
+
+    def place(i, q):
+        return i // SUB, pl.ds(pl.multiple_of(q * quarter + (i % SUB) * piece, piece), piece)
+
+    def w_y(i):
+        t, cut = place(i, b)
+        cols = pl.ds(pl.multiple_of(t * TILE, TILE), TILE)
+        return pltpu.make_async_remote_copy(
+            src_ref=w_ref.at[cut, cols], dst_ref=wv.at[tiles + t, cut],
+            send_sem=y_s.at[i], recv_sem=y_r.at[i], device_id=(b, yp), device_id_type=MESH)
+
+    def relay(i, q, send, recv, to):
+        t, cut = place(i, q)
+        there = wv.at[tiles + t, cut]
+        return pltpu.make_async_remote_copy(
+            src_ref=there, dst_ref=there, send_sem=send, recv_sem=recv,
+            device_id=(to, v), device_id_type=MESH)
+
+    def w_x(i, q):
+        return relay(i, q, x_s.at[i], x_r.at[i], xb)
+
+    def w_d(i, q, k):
+        return relay(i, q, d_s.at[k, i], d_r.at[k, i], cb)
+
+    for k in range(CHUNKS):
+        @pl.when(z < n - 1)
+        def _():
+            up(z, k, True).start()
+
+        @pl.when(z > 0)
+        def _():
+            down(z, k, True).start()
+
+    @pl.loop(0, total)
+    def _(i):
+        w_y(i).start()
+
+    own_rows.wait()
+    for t in range(tiles):
+        own_w(t).wait()
+
+    def order(o):
+        low = z < 2
+        zz = jnp.where(low, z, n - 1 - z)
+        s = jnp.where(o == 0, zz, jnp.where(o == 1, 1 - zz, o))
+        return jnp.where(low, s, n - 1 - s)
+
+    def row_event(d, k):
+        below, above = z - d, z + d
+
+        @pl.when(below >= 0)
+        def _():
+            up(below, k).wait_recv()
+
+            @pl.when(z < n - 1)
+            def _():
+                up(below, k).start()
+
+        @pl.when(above < n)
+        def _():
+            down(above, k).wait_recv()
+
+            @pl.when(z > 0)
+            def _():
+                down(above, k).start()
+
+    def product(src, t):
+        lg[src, t] = jnp.dot(rows[src], wv[t], preferred_element_type=jnp.float32)
+
+    def trees():
+        r_id = lax.broadcasted_iota(jnp.int32, (LANES, LANES), 0)
+        n_id = lax.broadcasted_iota(jnp.int32, (LANES, LANES), 1)
+        for p in range(pairs):
+            up_of = par_ref[pl.ds(p, 1), :] == r_id
+            pick[p] = up_of.astype(jnp.float32).astype(jnp.bfloat16)
+            jump[p] = (up_of & (n_id % nodes != 0)).astype(jnp.float32).astype(jnp.bfloat16)
+            anc[p] = (r_id == n_id).astype(jnp.float32).astype(jnp.bfloat16)
+
+        @pl.loop(0, (nodes - 1).bit_length())
+        def _(k):
+            for p in range(pairs):
+                a, j = anc[p], jump[p]
+                more = jnp.dot(a, j, preferred_element_type=jnp.float32)
+                twice = jnp.dot(j, j, preferred_element_type=jnp.float32)
+                anc[p] = (a.astype(jnp.float32) + more).astype(jnp.bfloat16)
+                jump[p] = twice.astype(jnp.bfloat16)
+
+    steps = plan(tiles)
+    tasks, first = [], []
+    last_step = max(SUB * tiles + 2, 2 * CHUNKS * (n - 1) - 2)
+    for i in range(last_step + 1):
+        first.append(len(tasks))
+        tasks += steps.get(i, [])
+    first.append(len(tasks))
+
+    @pl.loop(0, last_step + 1)
+    def _(i):
+        @pl.when(i < total)
+        def _():
+            w_y(i).wait_recv()
+            w_x(i, b).start()
+            w_d(i, b, 0).start()
+
+        @pl.when((i >= 1) & (i <= total))
+        def _():
+            w_x(i - 1, xb).wait_recv()
+            w_d(i - 1, xb, 1).start()
+            w_d(i - 1, cb, 0).wait_recv()
+
+        @pl.when((i >= 2) & (i <= total + 1))
+        def _():
+            w_d(i - 2, cxb, 1).wait_recv()
+
+        @pl.when((i % 2 == 1) & (i < 2 * CHUNKS * (n - 1) - 1))
+        def _():
+            j = i // 2
+            row_event(j // CHUNKS + 1, j % CHUNKS)
+
+        @pl.when(i == 7)
+        def _():
+            trees()
+
+        def run(g, c):
+            o = table(g, [a for a, _ in tasks])
+            t = table(g, [a for _, a in tasks])
+            product(order(o), t)
+            return c
+
+        lax.fori_loop(table(i, first[:-1]), table(i, first[1:]), run, 0)
+
+    def stats(src):
+        here = 2 * src + y
+        draft = draft_ref[pl.ds(here, 1), :]
+
+        def top(t, m):
+            l = lg[src, t]
+            for k in range(0, TILE, LANES):
+                m = jnp.maximum(m, l[:, k:k + LANES])
+            return m
+
+        mx = lax.fori_loop(1, 2 * tiles, top, jnp.maximum(lg[src, 0, :, :LANES], lg[src, 0, :, LANES:2 * LANES]))
+        m = jnp.max(mx, axis=1, keepdims=True)
+        c_id = lax.broadcasted_iota(jnp.int32, (TILE, LANES), 0)
+
+        def body(t, carry):
+            s, g = carry
+            l = lg[src, t]
+            e = jnp.exp(l - m)
+            for k in range(0, TILE, LANES):
+                s = s + e[:, k:k + LANES]
+            base = jnp.where(t < tiles, v * width + t * TILE, yp * width + (t - tiles) * TILE)
+            hot = (c_id == draft - base).astype(jnp.float32).astype(jnp.bfloat16)
+            for a in split3(l):
+                g = g + jnp.dot(a, hot, preferred_element_type=jnp.float32)
+            return s, g
+
+        zero = jnp.zeros((count, LANES), jnp.float32)
+        s, g = lax.fori_loop(0, 2 * tiles, body, (zero, zero))
+        r_id = lax.broadcasted_iota(jnp.int32, (LANES, LANES), 0)
+        t_row = jnp.sum(jnp.where(par_ref[pl.ds(here, 1), :] == r_id, g, 0.0), axis=0, keepdims=True)
+        m_row = jnp.max(mx.T, axis=0, keepdims=True)
+        s_row = jnp.sum(s.T, axis=0, keepdims=True)
+        sub = lax.broadcasted_iota(jnp.int32, (8, LANES), 0)
+        st[v, src] = jnp.where(sub == 0, m_row, jnp.where(sub == 1, s_row, jnp.where(sub == 2, t_row, 0.0)))
+
+    @pl.loop(0, n)
+    def _(o):
+        src = order(o)
+
+        @pl.when(o == n - 1)
+        def _():
+            row_event(n - 1, CHUNKS - 1)
+
+            @pl.loop(0, 2 * tiles)
+            def _(t):
+                product(src, t)
+
+        stats(src)
+
+    def tell(k):
+        return pltpu.make_async_remote_copy(
+            src_ref=st.at[v], dst_ref=st.at[v], send_sem=st_s.at[k], recv_sem=st_r.at[v],
+            device_id=(b, lax.rem(v + k, peers)), device_id_type=MESH)
+
+    def heard(k):
+        other = lax.rem(v + k, peers)
+        return pltpu.make_async_remote_copy(
+            src_ref=st.at[other], dst_ref=st.at[other], send_sem=st_s.at[k], recv_sem=st_r.at[other],
+            device_id=(b, other), device_id_type=MESH)
+
+    for k in range(1, peers):
+        tell(k).start()
+
+    @pl.loop(0, total)
+    def _(i):
+        w_y(i).wait_send()
+        w_x(i, b).wait_send()
+        w_d(i, b, 0).wait_send()
+        w_d(i, xb, 1).wait_send()
+
+    @pl.loop(0, n)
+    def _(src):
+        @pl.loop(0, CHUNKS)
+        def _(k):
+            @pl.when((src <= z) & (z < n - 1))
+            def _():
+                up(src, k).wait_send()
+
+            @pl.when((src >= z) & (z > 0))
+            def _():
+                down(src, k).wait_send()
+
+    for k in range(1, peers):
+        heard(k).wait_recv()
+
+    sub = lax.broadcasted_iota(jnp.int32, (16, LANES), 0)
+    lane = lax.broadcasted_iota(jnp.int32, (1, LANES), 1)
+
+    def through(row, mat):
+        hi, mid, lo = [a.astype(jnp.float32) for a in split3(row)]
+        lhs = jnp.where(sub == 0, hi, jnp.where(sub == 1, mid, jnp.where(sub == 2, lo, 0.0)))
+        return jnp.sum(jnp.dot(lhs.astype(jnp.bfloat16), mat, preferred_element_type=jnp.float32), axis=0, keepdims=True)
+
+    for p in range(pairs):
+        src, yy = p // 2, p % 2
+        got = [st[2 * k + yy, src] for k in range(n)]
+        ms = [g[0:1] for g in got]
+        m = functools.reduce(jnp.maximum, ms)
+        s = sum(g[1:2] * jnp.exp(a - m) for g, a in zip(got, ms))
+        lt = m + jnp.log(s)
+        target = sum(g[2:3] for g in got)
+        dl = jnp.where(lane % nodes > 0, target - through(lt, pick[p]), 0.0)
+        ps = through(dl, anc[p])
+        for ref, row in ((lt_ref, lt), (dl_ref, dl), (ps_ref, ps)):
+            ref[pl.ds(2 * p, 1), :] = row[:, :nodes]
+            ref[pl.ds(2 * p + 1, 1), :] = pltpu.roll(row, nodes, 1)[:, :nodes]
+
+    for k in range(1, peers):
+        tell(k).wait_send()
+
+
+def per_device(n, hidden_rows, head_weight, draft_ids, parents):
+    seqs, nodes = draft_ids.shape
+    count, depth = hidden_rows.shape
+    tiles = head_weight.shape[1] // TILE
+    pairs = seqs // 2
+    drafts = draft_ids.reshape(pairs, 2 * nodes)
+    pars = (parents + nodes * (jnp.arange(seqs, dtype=jnp.int32) % 2)[:, None]).reshape(pairs, 2 * nodes)
+    out = jax.ShapeDtypeStruct((seqs, nodes), jnp.float32)
+    vmem = pl.BlockSpec(memory_space=pltpu.VMEM)
+    hbm = pl.BlockSpec(memory_space=pl.ANY)
+    dma = pltpu.SemaphoreType.DMA
+    total = tiles * SUB
+    return pl.pallas_call(
+        functools.partial(kernel, n, nodes),
+        out_shape=(out, out, out),
+        in_specs=[hbm, hbm, vmem, vmem],
+        out_specs=(vmem, vmem, vmem),
+        scratch_shapes=[
+            pltpu.VMEM((n, count, depth), jnp.bfloat16),
+            pltpu.VMEM((2 * tiles, depth, TILE), jnp.bfloat16),
+            pltpu.VMEM((n, 2 * tiles, count, TILE), jnp.float32),
+            pltpu.VMEM((2 * n, n, 8, LANES), jnp.float32),
+            pltpu.VMEM((pairs, LANES, LANES), jnp.bfloat16),
+            pltpu.VMEM((pairs, LANES, LANES), jnp.bfloat16),
+            pltpu.VMEM((pairs, LANES, LANES), jnp.bfloat16),
+            dma((n, CHUNKS)), dma((n, CHUNKS)), dma((n, CHUNKS)),
+            dma((total,)), dma((total,)), dma((total,)), dma((total,)),
+            dma((2, total)), dma((2, total)),
+            dma((2 * n,)), dma((2 * n,)),
+            dma((tiles,)), dma,
+        ],
+        compiler_params=pltpu.CompilerParams(
+            collective_id=0, has_side_effects=True, vmem_limit_bytes=56 * 1024 * 1024
+        ),
+    )(hidden_rows, head_weight, drafts, pars)
+
+
 def solution(mesh):
     placed = (P(("batch", "vocab"), None), P(None, "vocab"), P("batch", None), P("batch", None))
+    batch, vocab = mesh.shape["batch"], mesh.shape["vocab"]
+
+    def choose(hidden_rows, head_weight, draft_ids, parents):
+        count = hidden_rows.shape[0]
+        fits = batch == 4 and vocab == 8 and count == 2 * draft_ids.shape[1] == LANES
+        fits = fits and head_weight.shape[1] == 5 * TILE
+        if fits:
+            return per_device(vocab // 2, hidden_rows, head_weight, draft_ids, parents)
+        return general(hidden_rows, head_weight, draft_ids, parents)
+
     return jax.shard_map(
-        per_device,
+        choose,
         mesh=mesh,
         in_specs=placed,
         out_specs=(P("batch", None), P("batch", None), P("batch", None)),

time: 246 us -> 105 us (0.43)
  waiting for transfers between devices: 124 us -> 0 us
  Pallas kernels: 0 us -> 97.1 us
  blocking collectives: 52 us -> 0 us
  matrix products: 28 us -> 0 us
  local copies, waits for them, and re-layouts: 20.9 us -> 5.91 us
  between operations: 14.1 us -> 0.65 us
  other arithmetic: 5.6 us -> 0.77 us
    all_gather x1 -> x0, waiting for transfers between devices: 124 us -> none  [per_device(): gathered = lax.all_gather(hidden_rows, 'vocab', axis=0, tiled=True)]
    pallas_call x0 -> x1, Pallas kernels: none -> 97.1 us  [per_device(): pl.pallas_call(functools.partial(kernel, n, nodes), out_shape=(out, out,...]
    psum x1 -> x0, blocking collectives: 33.6 us -> none  [per_device(): row_total, target = lax.psum((local_sum, local_target), 'vocab')]
    dot_general x13 -> x0, matrix products: 28 us -> none  [the longest x1 18.1 us: per_device(): logits = jnp.dot(gathered, head_weight, preferred_element_type=jnp.float32)]
    pmax x1 -> x0, blocking collectives: 18.3 us -> none  [per_device(): row_top = lax.pmax(local_max, 'vocab')]
    gather x1 -> x0, local copies, waits for them, and re-layouts: 13.3 us -> none  [per_device(): jnp.take(logits.reshape(-1), parent_rows * shard_width + jnp.clip(columns...]
    reshape x4 -> x2, local copies, waits for them, and re-layouts: 7.3 us -> 2.02 us  [the longest x1 1.36 us: per_device(): drafts = draft_ids.reshape(pairs, 2 * nodes)]
    unnamed x4 -> x3, local copies, waits for them, and re-layouts: 0.01 us -> 3.89 us
  transfers between devices with their start and end apart: 1 -> 0, of which waited for: 1 -> 0; matrix products, arithmetic and copies ran while one was open for 2% -> 0% of each run, Pallas kernels for 0% -> 0%
where the time goes in v1:
time: 105 us; the launch traced here: 104 us
  Pallas kernels  97.1 us (92%)
  local copies, waits for them, and re-layouts  5.91 us (6%)
    pallas_call x1, Pallas kernels, per_device(): pl.pallas_call(functools.partial(kernel, n, nodes), out_shape=(out, out,...  97.1 us
    unnamed x3, local copies, waits for them, and re-layouts  3.89 us

profile of v1, /device:TPU:0, one launch (start us, length us, event | category | flops | bytes accessed | tf_op | source)
XLA Modules:
  0.0 104.4 jit_solution(8057280361458352336)
XLA Ops:
  0.6 1.4 %reshape.23.draft_ref = s32[8,128]{1,0:T(8,128)} reshape(s32[16,64]{1,0:T(8,128)} %param.6) | data formatting | bytes 8192 | tf_op jit(solution)/shard_map/reshape | solution.py:377
  2.0 0.8 broadcast_add_fusion
  2.8 0.7 reshape.24.par_ref
  3.4 97.1 %shard_map.67 = (f32[16,64]{1,0:T(8,128)}, f32[16,64]{1,0:T(8,128)}, f32[16,64]{1,0:T(8,128)}) custom-call(bf16[128,4096]{1,0:T(8,128)(2,1)} %h_ref.1, bf16[4096,1280]{1,0:T(8,128)(2,1)} %w_ref.1, s32[8,128]{1,0:T(8,128)} %reshape.23.draft_ref, s32[8,128]{1,0:T(8,128)} %reshape.24.par_ref), custom_call_target="tpu_custom_call" | custom-call | tf_op jit(solution)/shard_map/pallas_call | solution.py:384
  100.5 1.3 %copy.10 = f32[16,64]{1,0:T(8,128)} copy(f32[16,64]{1,0:T(8,128)} %get-tuple-element.6) | data formatting | bytes 8192
  101.8 1.3 %copy.11 = f32[16,64]{1,0:T(8,128)} copy(f32[16,64]{1,0:T(8,128)} %get-tuple-element.7) | data formatting | bytes 8192
  103.1 1.3 %copy.12 = f32[16,64]{1,0:T(8,128)} copy(f32[16,64]{1,0:T(8,128)} %get-tuple-element.8) | data formatting | bytes 8192
  (1 shorter events, 0.0 us)

commit v2 on v1

--- a/solution.py
+++ b/solution.py
@@ -73,6 +73,11 @@
     return out
 
 
+def split2(x):
+    hi = x.astype(jnp.bfloat16)
+    return hi, (x - hi.astype(jnp.float32)).astype(jnp.bfloat16)
+
+
 def split3(x):
     hi = x.astype(jnp.bfloat16)
     rest = x - hi.astype(jnp.float32)
@@ -81,8 +86,8 @@
     return hi, mid, lo
 
 
-def kernel(n, nodes, h_ref, w_ref, draft_ref, par_ref, lt_ref, dl_ref, ps_ref,
-           rows, wv, lg, st, pick, anc, jump,
+def kernel(n, nodes, h_ref, w_ref, ids_ref, up_ref, lt_ref, dl_ref, ps_ref,
+           draft_ref, par_ref, rows, wv, lg, mxa, gac, st, pick, anc, jump,
            up_s, dn_s, r_r, y_s, y_r, x_s, x_r, d_s, d_r, st_s, st_r, loc_w, loc_r):
     b, v = lax.axis_index("batch"), lax.axis_index("vocab")
     x, z, y = b // 2, v // 2, v % 2
@@ -165,6 +170,31 @@
     def _(i):
         w_y(i).start()
 
+    for p in range(pairs):
+        one, two = pl.ds(2 * p, 1), pl.ds(2 * p + 1, 1)
+        draft_ref[p:p + 1, :nodes] = ids_ref[one, :]
+        draft_ref[p:p + 1, nodes:] = ids_ref[two, :]
+        par_ref[p:p + 1, :nodes] = up_ref[one, :]
+        par_ref[p:p + 1, nodes:] = up_ref[two, :] + nodes
+    mxa[...] = jnp.full_like(mxa, -jnp.inf)
+    gac[...] = jnp.zeros_like(gac)
+    r_id = lax.broadcasted_iota(jnp.int32, (LANES, LANES), 0)
+    n_id = lax.broadcasted_iota(jnp.int32, (LANES, LANES), 1)
+    for p in range(pairs):
+        up_of = par_ref[pl.ds(p, 1), :] == r_id
+        pick[p] = up_of.astype(jnp.float32).astype(jnp.bfloat16)
+        jump[p] = (up_of & (n_id % nodes != 0)).astype(jnp.float32).astype(jnp.bfloat16)
+        anc[p] = (r_id == n_id).astype(jnp.float32).astype(jnp.bfloat16)
+
+    @pl.loop(0, (nodes - 1).bit_length())
+    def _(k):
+        for p in range(pairs):
+            a, j = anc[p], jump[p]
+            more = jnp.dot(a, j, preferred_element_type=jnp.float32)
+            twice = jnp.dot(j, j, preferred_element_type=jnp.float32)
+            anc[p] = (a.astype(jnp.float32) + more).astype(jnp.bfloat16)
+            jump[p] = twice.astype(jnp.bfloat16)
+
     own_rows.wait()
     for t in range(tiles):
         own_w(t).wait()
@@ -194,30 +224,25 @@
             def _():
                 down(above, k).start()
 
-    def product(src, t):
-        lg[src, t] = jnp.dot(rows[src], wv[t], preferred_element_type=jnp.float32)
-
-    def trees():
-        r_id = lax.broadcasted_iota(jnp.int32, (LANES, LANES), 0)
-        n_id = lax.broadcasted_iota(jnp.int32, (LANES, LANES), 1)
-        for p in range(pairs):
-            up_of = par_ref[pl.ds(p, 1), :] == r_id
-            pick[p] = up_of.astype(jnp.float32).astype(jnp.bfloat16)
-            jump[p] = (up_of & (n_id % nodes != 0)).astype(jnp.float32).astype(jnp.bfloat16)
-            anc[p] = (r_id == n_id).astype(jnp.float32).astype(jnp.bfloat16)
-
-        @pl.loop(0, (nodes - 1).bit_length())
-        def _(k):
-            for p in range(pairs):
-                a, j = anc[p], jump[p]
-                more = jnp.dot(a, j, preferred_element_type=jnp.float32)
-                twice = jnp.dot(j, j, preferred_element_type=jnp.float32)
-                anc[p] = (a.astype(jnp.float32) + more).astype(jnp.bfloat16)
-                jump[p] = twice.astype(jnp.bfloat16)
+    def product(src, t, low=0, size=None):
+        size = size or count
+        cut = pl.ds(low, size)
+        l = jnp.dot(rows[src, cut, :], wv[t], preferred_element_type=jnp.float32)
+        lg[src, t, cut, :] = l
+        m = mxa[src, cut, :]
+        for k in range(0, TILE, LANES):
+            m = jnp.maximum(m, l[:, k:k + LANES])
+        mxa[src, cut, :] = m
+        here = 2 * src + y
+        base = jnp.where(t < tiles, v * width + t * TILE, yp * width + (t - tiles) * TILE)
+        c_id = lax.broadcasted_iota(jnp.int32, (TILE, LANES), 0)
+        hot = (c_id == draft_ref[pl.ds(here, 1), :] - base).astype(jnp.float32).astype(jnp.bfloat16)
+        both = jnp.dot(jnp.concatenate(split2(l), axis=0), hot, preferred_element_type=jnp.float32)
+        gac[src, cut, :] += both[:size] + both[size:]
 
     steps = plan(tiles)
     tasks, first = [], []
-    last_step = max(SUB * tiles + 2, 2 * CHUNKS * (n - 1) - 2)
+    last_step = max(SUB * tiles + 1, 2 * (CHUNKS * (n - 1) - 2) - 1)
     for i in range(last_step + 1):
         first.append(len(tasks))
         tasks += steps.get(i, [])
@@ -241,14 +266,10 @@
         def _():
             w_d(i - 2, cxb, 1).wait_recv()
 
-        @pl.when((i % 2 == 1) & (i < 2 * CHUNKS * (n - 1) - 1))
+        @pl.when((i % 2 == 1) & (i < 2 * (CHUNKS * (n - 1) - 2)))
         def _():
             j = i // 2
             row_event(j // CHUNKS + 1, j % CHUNKS)
-
-        @pl.when(i == 7)
-        def _():
-            trees()
 
         def run(g, c):
             o = table(g, [a for a, _ in tasks])
@@ -260,52 +281,42 @@
 
     def stats(src):
         here = 2 * src + y
-        draft = draft_ref[pl.ds(here, 1), :]
-
-        def top(t, m):
-            l = lg[src, t]
-            for k in range(0, TILE, LANES):
-                m = jnp.maximum(m, l[:, k:k + LANES])
-            return m
-
-        mx = lax.fori_loop(1, 2 * tiles, top, jnp.maximum(lg[src, 0, :, :LANES], lg[src, 0, :, LANES:2 * LANES]))
+        mx = mxa[src]
         m = jnp.max(mx, axis=1, keepdims=True)
-        c_id = lax.broadcasted_iota(jnp.int32, (TILE, LANES), 0)
-
-        def body(t, carry):
-            s, g = carry
-            l = lg[src, t]
-            e = jnp.exp(l - m)
-            for k in range(0, TILE, LANES):
-                s = s + e[:, k:k + LANES]
-            base = jnp.where(t < tiles, v * width + t * TILE, yp * width + (t - tiles) * TILE)
-            hot = (c_id == draft - base).astype(jnp.float32).astype(jnp.bfloat16)
-            for a in split3(l):
-                g = g + jnp.dot(a, hot, preferred_element_type=jnp.float32)
-            return s, g
-
-        zero = jnp.zeros((count, LANES), jnp.float32)
-        s, g = lax.fori_loop(0, 2 * tiles, body, (zero, zero))
+        sums = []
+        for r in range(0, count, 32):
+            s = jnp.zeros((32, LANES), jnp.float32)
+            for t in range(2 * tiles):
+                for k in range(0, TILE, LANES):
+                    s = s + jnp.exp(lg[src, t, r:r + 32, k:k + LANES] - m[r:r + 32])
+            sums.append(s)
+        s = jnp.concatenate(sums, axis=0)
         r_id = lax.broadcasted_iota(jnp.int32, (LANES, LANES), 0)
-        t_row = jnp.sum(jnp.where(par_ref[pl.ds(here, 1), :] == r_id, g, 0.0), axis=0, keepdims=True)
+        t_row = jnp.sum(jnp.where(par_ref[pl.ds(here, 1), :] == r_id, gac[src], 0.0), axis=0, keepdims=True)
         m_row = jnp.max(mx.T, axis=0, keepdims=True)
         s_row = jnp.sum(s.T, axis=0, keepdims=True)
         sub = lax.broadcasted_iota(jnp.int32, (8, LANES), 0)
         st[v, src] = jnp.where(sub == 0, m_row, jnp.where(sub == 1, s_row, jnp.where(sub == 2, t_row, 0.0)))
 
+    last = order(n - 1)
+    half = count // 2
+
+    @pl.loop(0, 2 * tiles)
+    def _(t):
+        product(last, t, 0, half)
+
     @pl.loop(0, n)
     def _(o):
-        src = order(o)
-
         @pl.when(o == n - 1)
         def _():
+            row_event(n - 1, CHUNKS - 2)
             row_event(n - 1, CHUNKS - 1)
 
             @pl.loop(0, 2 * tiles)
             def _(t):
-                product(src, t)
-
-        stats(src)
+                product(last, t, half, half)
+
+        stats(order(o))
 
     def tell(k):
         return pltpu.make_async_remote_copy(
@@ -369,27 +380,35 @@
         tell(k).wait_send()
 
 
+def hand_on(a_ref, b_ref, c_ref, x_ref, y_ref, z_ref):
+    x_ref[...] = a_ref[...]
+    y_ref[...] = b_ref[...]
+    z_ref[...] = c_ref[...]
+
+
 def per_device(n, hidden_rows, head_weight, draft_ids, parents):
     seqs, nodes = draft_ids.shape
     count, depth = hidden_rows.shape
     tiles = head_weight.shape[1] // TILE
     pairs = seqs // 2
-    drafts = draft_ids.reshape(pairs, 2 * nodes)
-    pars = (parents + nodes * (jnp.arange(seqs, dtype=jnp.int32) % 2)[:, None]).reshape(pairs, 2 * nodes)
     out = jax.ShapeDtypeStruct((seqs, nodes), jnp.float32)
     vmem = pl.BlockSpec(memory_space=pltpu.VMEM)
     hbm = pl.BlockSpec(memory_space=pl.ANY)
     dma = pltpu.SemaphoreType.DMA
     total = tiles * SUB
-    return pl.pallas_call(
+    found = pl.pallas_call(
         functools.partial(kernel, n, nodes),
         out_shape=(out, out, out),
         in_specs=[hbm, hbm, vmem, vmem],
         out_specs=(vmem, vmem, vmem),
         scratch_shapes=[
+            pltpu.VMEM((pairs, LANES), jnp.int32),
+            pltpu.VMEM((pairs, LANES), jnp.int32),
             pltpu.VMEM((n, count, depth), jnp.bfloat16),
             pltpu.VMEM((2 * tiles, depth, TILE), jnp.bfloat16),
             pltpu.VMEM((n, 2 * tiles, count, TILE), jnp.float32),
+            pltpu.VMEM((n, count, LANES), jnp.float32),
+            pltpu.VMEM((n, count, LANES), jnp.float32),
             pltpu.VMEM((2 * n, n, 8, LANES), jnp.float32),
             pltpu.VMEM((pairs, LANES, LANES), jnp.bfloat16),
             pltpu.VMEM((pairs, LANES, LANES), jnp.bfloat16),
@@ -403,7 +422,13 @@
         compiler_params=pltpu.CompilerParams(
             collective_id=0, has_side_effects=True, vmem_limit_bytes=56 * 1024 * 1024
         ),
-    )(hidden_rows, head_weight, drafts, pars)
+    )(hidden_rows, head_weight, draft_ids, parents)
+    return pl.pallas_call(
+        hand_on,
+        out_shape=(out, out, out),
+        in_specs=[vmem] * 3,
+        out_specs=(vmem, vmem, vmem),
+    )(*found)
 
 
 def solution(mesh):

time: 105 us -> 100 us (0.952)
  local copies, waits for them, and re-layouts: 5.91 us -> 0 us
  Pallas kernels: 97.1 us -> 99.3 us
    unnamed x3 -> x0, local copies, waits for them, and re-layouts: 3.89 us -> none
    reshape x2 -> x0, local copies, waits for them, and re-layouts: 2.02 us -> none  [the longest x1 1.36 us: per_device(): drafts = draft_ids.reshape(pairs, 2 * nodes)]
    pallas_call x0 -> x1, Pallas kernels: none -> 1.34 us  [per_device(): pl.pallas_call(hand_on, out_shape=(out, out, out), in_specs=[vmem] * 3, o...]
where the time goes in v2:
time: 100 us; the launch traced here: 99.9 us
  Pallas kernels  99.3 us (99%)
    pallas_call x1, Pallas kernels, per_device(): pl.pallas_call(functools.partial(kernel, n, nodes), out_shape=(out, out,...  97.9 us

profile of v2, /device:TPU:0, one launch (start us, length us, event | category | flops | bytes accessed | tf_op | source)
XLA Modules:
  0.0 99.9 jit_solution(1418190077239107980)
XLA Ops:
  0.6 97.9 %shard_map.67 = (f32[16,64]{1,0:T(8,128)}, f32[16,64]{1,0:T(8,128)}, f32[16,64]{1,0:T(8,128)}) custom-call(bf16[128,4096]{1,0:T(8,128)(2,1)} %h_ref.1, bf16[4096,1280]{1,0:T(8,128)(2,1)} %w_ref.1, s32[16,64]{1,0:T(8,128)} %ids_ref.1, s32[16,64]{1,0:T(8,128)} %up_ref.1), custom_call_target="tpu_custom_call" | custom-call | tf_op jit(solution)/shard_map/pallas_call | solution.py:399
  98.6 1.3 %shard_map.68 = (f32[16,64]{1,0:T(8,128)}, f32[16,64]{1,0:T(8,128)}, f32[16,64]{1,0:T(8,128)}) custom-call(f32[16,64]{1,0:T(8,128)} %get-tuple-element.6.a_ref, f32[16,64]{1,0:T(8,128)} %get-tuple-element.7.b_ref, f32[16,64]{1,0:T(8,128)} %get-tuple-element.8.c_ref), custom_call_target="tpu_custom_call" | custom-call | tf_op jit(solution)/shard_map/pallas_call | solution.py:426

commit v3 on v2

--- a/solution.py
+++ b/solution.py
@@ -112,7 +112,7 @@
     pl.semaphore_signal(barrier, inc=1, device_id=(xb, v), device_id_type=MESH)
 
     def own_w(t):
-        return pltpu.make_async_copy(w_ref.at[:, pl.ds(t * TILE, TILE)], wv.at[t], loc_w.at[t])
+        return pltpu.make_async_copy(w_ref.at[:, pl.ds(pl.multiple_of(t * TILE, TILE), TILE)], wv.at[t], loc_w.at[t])
 
     own_rows = pltpu.make_async_copy(h_ref, rows.at[z], loc_r)
     own_rows.start()
@@ -186,8 +186,7 @@
         jump[p] = (up_of & (n_id % nodes != 0)).astype(jnp.float32).astype(jnp.bfloat16)
         anc[p] = (r_id == n_id).astype(jnp.float32).astype(jnp.bfloat16)
 
-    @pl.loop(0, (nodes - 1).bit_length())
-    def _(k):
+    def double():
         for p in range(pairs):
             a, j = anc[p], jump[p]
             more = jnp.dot(a, j, preferred_element_type=jnp.float32)
@@ -196,8 +195,6 @@
             jump[p] = twice.astype(jnp.bfloat16)
 
     own_rows.wait()
-    for t in range(tiles):
-        own_w(t).wait()
 
     def order(o):
         low = z < 2
@@ -224,21 +221,28 @@
             def _():
                 down(above, k).start()
 
-    def product(src, t, low=0, size=None):
-        size = size or count
-        cut = pl.ds(low, size)
-        l = jnp.dot(rows[src, cut, :], wv[t], preferred_element_type=jnp.float32)
-        lg[src, t, cut, :] = l
-        m = mxa[src, cut, :]
-        for k in range(0, TILE, LANES):
-            m = jnp.maximum(m, l[:, k:k + LANES])
-        mxa[src, cut, :] = m
+    def picked(src, t, l):
         here = 2 * src + y
         base = jnp.where(t < tiles, v * width + t * TILE, yp * width + (t - tiles) * TILE)
         c_id = lax.broadcasted_iota(jnp.int32, (TILE, LANES), 0)
         hot = (c_id == draft_ref[pl.ds(here, 1), :] - base).astype(jnp.float32).astype(jnp.bfloat16)
         both = jnp.dot(jnp.concatenate(split2(l), axis=0), hot, preferred_element_type=jnp.float32)
-        gac[src, cut, :] += both[:size] + both[size:]
+        gac[src] += both[:count] + both[count:]
+
+    def keep(src, t, l):
+        lg[src, t] = l
+        m = mxa[src]
+        for k in range(0, TILE, LANES):
+            m = jnp.maximum(m, l[:, k:k + LANES])
+        mxa[src] = m
+
+    def logits(src, t):
+        return jnp.dot(rows[src], wv[t], preferred_element_type=jnp.float32)
+
+    def product(src, t):
+        l = logits(src, t)
+        keep(src, t, l)
+        picked(src, t, l)
 
     steps = plan(tiles)
     tasks, first = [], []
@@ -270,6 +274,14 @@
         def _():
             j = i // 2
             row_event(j // CHUNKS + 1, j % CHUNKS)
+
+        @pl.when((i >= 1) & (i <= tiles))
+        def _():
+            own_w(i - 1).wait()
+
+        @pl.when((i >= 2) & (i < 2 + (nodes - 1).bit_length()))
+        def _():
+            double()
 
         def run(g, c):
             o = table(g, [a for a, _ in tasks])
@@ -299,11 +311,6 @@
         st[v, src] = jnp.where(sub == 0, m_row, jnp.where(sub == 1, s_row, jnp.where(sub == 2, t_row, 0.0)))
 
     last = order(n - 1)
-    half = count // 2
-
-    @pl.loop(0, 2 * tiles)
-    def _(t):
-        product(last, t, 0, half)
 
     @pl.loop(0, n)
     def _(o):
@@ -312,9 +319,16 @@
             row_event(n - 1, CHUNKS - 2)
             row_event(n - 1, CHUNKS - 1)
 
-            @pl.loop(0, 2 * tiles)
+            keep(last, 0, logits(last, 0))
+
+            @pl.loop(1, 2 * tiles)
             def _(t):
-                product(last, t, half, half)
+                before = lg[last, t - 1]
+                l = logits(last, t)
+                picked(last, t - 1, before)
+                keep(last, t, l)
+
+            picked(last, 2 * tiles - 1, lg[last, 2 * tiles - 1])
 
         stats(order(o))
 

time: 100 us -> 93.1 us (0.931)
  Pallas kernels: 99.3 us -> 92.1 us
    pallas_call x1, Pallas kernels: 97.9 us -> 90.7 us  [per_device(): pl.pallas_call(functools.partial(kernel, n, nodes), out_shape=(out, out,...]
where the time goes in v3:
time: 93.1 us; the launch traced here: 92.7 us
  Pallas kernels  92.1 us (99%)
    pallas_call x1, Pallas kernels, per_device(): pl.pallas_call(functools.partial(kernel, n, nodes), out_shape=(out, out,...  90.7 us

profile of v3, /device:TPU:0, one launch (start us, length us, event | category | flops | bytes accessed | tf_op | source)
XLA Modules:
  0.0 92.7 jit_solution(1286509977129380155)
XLA Ops:
  0.6 90.7 %shard_map.67 = (f32[16,64]{1,0:T(8,128)}, f32[16,64]{1,0:T(8,128)}, f32[16,64]{1,0:T(8,128)}) custom-call(bf16[128,4096]{1,0:T(8,128)(2,1)} %h_ref.1, bf16[4096,1280]{1,0:T(8,128)(2,1)} %w_ref.1, s32[16,64]{1,0:T(8,128)} %ids_ref.1, s32[16,64]{1,0:T(8,128)} %up_ref.1), custom_call_target="tpu_custom_call" | custom-call | tf_op jit(solution)/shard_map/pallas_call | solution.py:413
  91.4 1.3 %shard_map.68 = (f32[16,64]{1,0:T(8,128)}, f32[16,64]{1,0:T(8,128)}, f32[16,64]{1,0:T(8,128)}) custom-call(f32[16,64]{1,0:T(8,128)} %get-tuple-element.6.a_ref, f32[16,64]{1,0:T(8,128)} %get-tuple-element.7.b_ref, f32[16,64]{1,0:T(8,128)} %get-tuple-element.8.c_ref), custom_call_target="tpu_custom_call" | custom-call | tf_op jit(solution)/shard_map/pallas_call | solution.py:440
